TPU v7x, 32 devices: a whole 2x2x4 slice. The times are simulated.
32 devices in a mesh: grp: 2 (over y), row: 16 (over z, x, core).
Axes of the slice: x: 2, y: 2, z: 4, core: 2. Of those that a mesh axis runs over, the one named last changes fastest.
Arguments:
- cells: float32 [256, 128, 192], P(('grp', 'row')), parts along dimension 0, may hold values from -6 to 6
- n_train: int32 [2], P('grp'), parts along dimension 0, may hold values from 16 to 127
- present: int32 [256], P('grp'), parts along dimension 0, may hold values from 0 to 1, as said below
- norm_gain: float32 [3, 192], replicated, may hold values from 0.1 to 1.9
- feat_qkv: bfloat16 [3, 192, 192], replicated, may hold values from -6 to 6
- feat_out: bfloat16 [192, 192], replicated, may hold values from -0.4375 to 0.4375
- item_qkv: bfloat16 [3, 192, 192], replicated, may hold values from -6 to 6
- item_out: bfloat16 [192, 192], replicated, may hold values from -0.875 to 0.875
- mlp_in: bfloat16 [192, 768], replicated, may hold values from -0.4375 to 0.4375
- mlp_out: bfloat16 [768, 192], replicated, may hold values from -0.21875 to 0.21875
Outputs:
- result: float32 [256, 128, 192], P(('grp', 'row')), parts along dimension 0
There are 2 independent parts, one for each index of `grp`. A program takes and returns all parts, laid end to end along the dimension named above; an argument that names none is the same for every part. Nothing has to cross between parts.
Inputs may be any that keep to these rules, and one draw needn't show every extreme that they name: At least one of the 128 features is present.
All inputs are finite; a program needn't handle non-finite values.
Results may differ from a plain program's by a relative error of at most 0.03.
The roundings to bfloat16 on the way count: a program that leaves them out, or rounds other values in their place, can miss the bound.
Values may be sent and summed in bfloat16 or wider, within the bound.
A program may use at most 64 MiB of HBM per device.

v0:
```python
import math

import jax
import jax.numpy as jnp
from jax import lax
from jax.sharding import PartitionSpec as P

HEADS = 6


norm_floor = 0.25
masked_score = -1e30


def layer_norm(stream, gain):
    average = jnp.mean(stream, axis=-1, keepdims=True)
    centred = stream - average
    spread = jnp.mean(centred * centred, axis=-1, keepdims=True)
    return centred * lax.rsqrt(spread + norm_floor) * gain


def softmax_rows(scores):
    largest = jnp.max(scores, axis=-1, keepdims=True)
    exponent = jnp.exp(scores - largest)
    return exponent / jnp.sum(exponent, axis=-1, keepdims=True)


def body(
    cells, n_train, present, norm_gain, feat_qkv, feat_out, item_qkv, item_out, mlp_in, mlp_out
):
    row_dev, feature_count, model_width = cells.shape
    devices_row = lax.axis_size("row")
    total_rows = row_dev * devices_row
    feat_dev = feature_count // devices_row
    head_size = model_width // HEADS
    scale = 1.0 / math.sqrt(head_size)
    query_rows = min(512, total_rows)
    highest = lax.Precision.HIGHEST
    normed = layer_norm(cells, norm_gain[0]).astype(jnp.bfloat16)
    triplet = jnp.einsum("rfe,ced->crfd", normed, feat_qkv, preferred_element_type=jnp.float32)
    triplet = triplet.reshape(3, row_dev, feature_count, HEADS, head_size)
    feat_values = triplet[2].astype(jnp.bfloat16)
    scores = jnp.einsum("rfhd,rghd->rhfg", triplet[0], triplet[1], precision=highest) * scale
    scores = jnp.where(present[None, None, None, :] > 0, scores, masked_score)
    weights = softmax_rows(scores).astype(jnp.bfloat16)
    context = jnp.einsum(
        "rhfg,rghd->rfhd", weights, feat_values, preferred_element_type=jnp.float32
    ).astype(jnp.bfloat16)
    context = context.reshape(row_dev, feature_count, model_width)
    cells_mid = cells + jnp.dot(context, feat_out, preferred_element_type=jnp.float32)
    key_live = lax.iota(jnp.int32, total_rows) < n_train[0]
    arrived = lax.all_to_all(
        cells_mid.reshape(row_dev, devices_row, feat_dev, model_width).astype(jnp.bfloat16),
        "row",
        split_axis=1,
        concat_axis=0,
        tiled=True,
    ).astype(jnp.float32)
    members = arrived.shape[2]
    stream = arrived.reshape(total_rows, members, model_width)
    normed_rows = layer_norm(stream, norm_gain[1]).astype(jnp.bfloat16)
    triples = jnp.einsum("rke,ced->kcrd", normed_rows, item_qkv, preferred_element_type=jnp.float32)

    def one_feature(triple):
        keys = triple[1].reshape(total_rows, HEADS, head_size)
        values = triple[2].astype(jnp.bfloat16).reshape(total_rows, HEADS, head_size)
        queries = triple[0].reshape(total_rows // query_rows, query_rows, HEADS, head_size)

        def query_group(chosen):
            group_scores = jnp.einsum("qhd,shd->hqs", chosen, keys, precision=highest) * scale
            group_scores = jnp.where(key_live[None, None, :], group_scores, masked_score)
            group_weights = softmax_rows(group_scores).astype(jnp.bfloat16)
            return jnp.einsum(
                "hqs,shd->qhd", group_weights, values, preferred_element_type=jnp.float32
            ).astype(jnp.bfloat16)

        return lax.map(query_group, queries).reshape(total_rows, model_width)

    gathered = lax.map(one_feature, triples)
    late = stream + jnp.dot(
        jnp.transpose(gathered, (1, 0, 2)), item_out, preferred_element_type=jnp.float32
    )
    normed_late = layer_norm(late, norm_gain[2]).astype(jnp.bfloat16)
    hidden = jax.nn.gelu(
        jnp.dot(normed_late, mlp_in, preferred_element_type=jnp.float32), approximate=False
    ).astype(jnp.bfloat16)
    updated = late + jnp.dot(hidden, mlp_out, preferred_element_type=jnp.float32)
    returned = lax.all_to_all(
        updated.reshape(total_rows, 1, members, model_width).astype(jnp.bfloat16),
        "row",
        split_axis=0,
        concat_axis=1,
        tiled=True,
    ).astype(jnp.float32)
    return returned.reshape(row_dev, feature_count, model_width)


def solution(mesh):
    return jax.shard_map(
        body,
        mesh=mesh,
        in_specs=(
            P(("grp", "row"), None, None),
            P("grp"),
            P("grp"),
            P(),
            P(),
            P(),
            P(),
            P(),
            P(),
            P(),
        ),
        out_specs=P(("grp", "row"), None, None),
        check_vma=False,
    )
```

profile of v0, /device:TPU:0, one launch (start us, length us, event | category | flops | bytes accessed | tf_op | source)
XLA Modules:
  0.0 84.8 jit_solution(5681295314958573850)
XLA Ops:
  0.0 0.8 fusion.94
  0.8 1.2 %reduce_sum.73 = f32[8,128]{1,0:T(8,128)S(1)} reduce(f32[8,128,192]{1,2,0:T(8,128)} %param.12, f32[]{:T(128)} %constant.51.clone.1), dimensions={2}, to_apply=%region_0.0 | reduce | flops 195584 | bytes 790532 | tf_op jit(solution)/shard_map/reduce_sum | solution.py:16
  2.0 1.2 %multiply_reduce_fusion.1 = f32[8,128]{1,0:T(8,128)S(1)} fusion(f32[8,128,192]{1,2,0:T(8,128)} %param.12, f32[8,128]{1,0:T(8,128)S(1)} %broadcast_multiply_fusion.2), kind=kLoop, calls=%fused_computation.66 | loop fusion | flops 588800 | bytes 794624 | tf_op jit(solution)/shard_map/reduce_sum | solution.py:18
  3.2 1.8 %convolution_bitcast_fusion.1 = f32[3,8,128,192]{2,3,0,1:T(8,128)S(1)} fusion(f32[8,128,192]{1,2,0:T(8,128)} %param.12, f32[192]{0:T(256)S(1)} %bitcast.123, f32[8,128]{1,0:T(8,128)S(1)} %add_rsqrt_fusion.2, f32[8,128]{1,0:T(8,128)S(1)} %broadcast_multiply_fusion.2, bf16[3,192,192]{2,1,0:T(8,128)(2,1)} %param.16), kind=kOutput, calls=%fused_computation.42 | convolution fusion | flops 227278848 | bytes 3375872 | tf_op jit(solution)/shard_map/rfe,ced->crfd/dot_general | solution.py:40
  5.3 5.1 %fusion.97 = f32[8,6,128,128]{2,3,1,0:T(8,128)S(1)} fusion(f32[8,128,6,32]{1,3,2,0:T(8,128)S(1)} %bitcast.114, f32[8,128,6,32]{1,3,2,0:T(8,128)S(1)} %bitcast.113), kind=kOutput, calls=%fused_computation.134 | convolution fusion | flops 301989888 | bytes 4718592 | tf_op jit(solution)/shard_map/rfhd,rghd->rhfg/dot_general | solution.py:43
  10.4 1.2 %fusion.95 = (f32[8,6,128]{2,1,0:T(8,128)S(1)}, f32[8,6,128,128]{2,3,1,0:T(8,128)S(1)}) fusion(f32[8,6,128,128]{2,3,1,0:T(8,128)S(1)} %fusion.97, pred[128]{0:T(512)(128)(4,1)S(1)} %broadcast_compare_fusion), kind=kOutput, calls=%fused_computation.132 | output fusion | flops 4718719 | bytes 6316160 | tf_op jit(solution)/shard_map/sub | solution.py:24
  13.2 0.8 copy.60
  14.1 7.4 %all-to-all-start = ((bf16[8,16,8,192]{3,2,0,1:T(8,128)(2,1)}), bf16[8,16,8,192]{3,2,0,1:T(8,128)(2,1)S(1)}, u32[]{:S(2)}, u32[]{:S(2)}) async-start(bf16[8,16,8,192]{3,2,0,1:T(8,128)(2,1)} %copy.60), calls=%async_computation | async-start | bytes 1048576 | tf_op jit(solution)/shard_map/all_to_all | solution.py:52
  21.5 14.2 %all-to-all-done = bf16[8,16,8,192]{3,2,0,1:T(8,128)(2,1)S(1)} async-done(((bf16[8,16,8,192]{3,2,0,1:T(8,128)(2,1)}), bf16[8,16,8,192]{3,2,0,1:T(8,128)(2,1)S(1)}, u32[]{:S(2)}, u32[]{:S(2)}) %all-to-all-start) | async-done | bytes 393248 | tf_op jit(solution)/shard_map/all_to_all | solution.py:52
  35.9 1.3 %copy.73 = f32[128,8,192]{0,2,1:T(8,128)} copy(f32[128,8,192]{2,1,0:T(8,128)S(1)} %bitcast.112) | data formatting | bytes 1572864 | tf_op jit(solution)/shard_map/convert_element_type | solution.py:58
  39.1 15.0 %while.11 = (s32[]{:T(128)}, bf16[8,128,192]{1,2,0:T(8,128)(2,1)S(1)}, f32[8,3,128,192]{2,3,1,0:T(8,128)S(1)}, s32[]{:T(128)}, s32[]{:T(128)}, /*index=5*/s32[]{:T(128)}, s32[]{}, s32[]{}) while((s32[]{:T(128)}, bf16[8,128,192]{1,2,0:T(8,128)(2,1)S(1)}, f32[8,3,128,192]{2,3,1,0:T(8,128)S(1)}, s32[]{:T(128)}, s32[]{:T(128)}, ...), condition=%wide.region_9.10_spmd.clone, body=%wide.region_6.9_spmd.clone.sunk | while | flops 44754052 | bytes 2070925 | solution.py:79
  39.8 0.8 fusion.119
  41.7 0.8 fusion.119
  43.5 0.8 fusion.119
  45.4 0.8 fusion.119
  47.3 0.8 fusion.119
  49.1 0.8 fusion.119
  51.0 0.8 fusion.119
  52.9 0.8 fusion.119
  54.0 1.5 %fusion.96 = (f32[128,8]{0,1:T(8,128)S(1)}, f32[128,8,192]{0,2,1:T(8,128)S(1)}) fusion(f32[128,8,192]{0,2,1:T(8,128)} %copy.73, bf16[192,192]{1,0:T(8,128)(2,1)} %param.19, bf16[8,128,192]{1,2,0:T(8,128)(2,1)S(1)} %get-tuple-element.45), kind=kOutput, calls=%fused_computation.133 | convolution fusion | flops 75889664 | bytes 2043904 | tf_op jit(solution)/shard_map/dot_general | solution.py:80
  55.7 1.5 %fusion.38 = (u8[128,768]{1,0:T(8,128)(4,1)S(1)}, u8[128,768]{1,0:T(8,128)(4,1)S(1)}, f32[128,8,768]{2,0,1:T(8,128)S(1)}) fusion(bf16[192,768]{1,0:T(8,128)(2,1)S(1)} %copy-done, f32[128,8,192]{0,2,1:T(8,128)S(1)} %get-tuple-element.77, f32[192]{0:T(256)S(1)} %bitcast.125, f32[128,8]{0,1:T(8,128)S(1)} %add_rsqrt_fusion.1, ...), kind=kOutput, calls=%fused_computation.68 | convolution fusion | flops 312803328 | bytes 4432640 | tf_op jit(solution)/shard_map/dot_general | solution.py:85
  57.2 7.7 %fusion.32 = bf16[128,1,8,192]{0,3,2,1:T(8,128)(2,1)S(1)} fusion(f32[128,8,192]{0,2,1:T(8,128)S(1)} %get-tuple-element.77, f32[128,8,768]{2,0,1:T(8,128)S(1)} %get-tuple-element.78, u8[128,768]{1,0:T(8,128)(4,1)S(1)} %get-tuple-element.58, u8[128,768]{1,0:T(8,128)(4,1)S(1)} %get-tuple-element.57, bf16[768,192]{0,1:T(8,128)(2,1)S(1)} %copy-done.4), kind=kOutput, calls=%fused_computation.54 | convolution fusion | flops 357433344 | bytes 4816896 | tf_op jit(solution)/shard_map/dot_general | solution.py:87
  65.3 18.2 %all_to_all.8 = bf16[128,1,8,192]{3,2,1,0:T(8,128)(2,1)S(1)} all-to-all(bf16[128,1,8,192]{3,2,1,0:T(8,128)(2,1)S(1)} %copy.74), channel_id=1, replica_groups=mesh['grp'=2,'row'=16] {'row'}, dimensions={0} | all-to-all | bytes 786432 | tf_op jit(solution)/shard_map/all_to_all | solution.py:88
  83.6 1.2 %copy.77 = f32[8,128,192]{1,2,0:T(8,128)} copy(f32[8,128,192]{2,1,0:T(8,128)S(1)} %copy_bitcast_fusion) | data formatting | bytes 1572864 | tf_op jit(solution)/shard_map/convert_element_type | solution.py:94
  (85 shorter events, 12.6 us)
Async XLA Ops:
  0.0 55.7 %copy-start = (bf16[192,768]{1,0:T(8,128)(2,1)S(1)}, bf16[192,768]{1,0:T(8,128)(2,1)}, u32[]{:S(2)}) copy-start(bf16[192,768]{1,0:T(8,128)(2,1)} %param.20) | copy-start | bytes 884740
  3.2 2.0 %copy-start.5 = (s32[128]{0:T(128)S(1)}, s32[128]{0:T(128)}, u32[]{:S(2)}) copy-start(s32[128]{0:T(128)} %param.14) | copy-start | bytes 1540
  11.6 1.1 %copy-start.1 = (f32[8,128,192]{1,2,0:T(8,128)S(1)}, f32[8,128,192]{1,2,0:T(8,128)}, u32[]{:S(2)}) copy-start(f32[8,128,192]{1,2,0:T(8,128)} %param.12) | copy-start | bytes 2359300
  11.6 1.1 %copy-start.3 = (bf16[192,192]{1,0:T(8,128)(2,1)S(1)}, bf16[192,192]{1,0:T(8,128)(2,1)}, u32[]{:S(2)}) copy-start(bf16[192,192]{1,0:T(8,128)(2,1)} %param.17) | copy-start | bytes 221188
  14.1 21.7 %all-to-all-start = ((bf16[8,16,8,192]{3,2,0,1:T(8,128)(2,1)}), bf16[8,16,8,192]{3,2,0,1:T(8,128)(2,1)S(1)}, u32[]{:S(2)}, u32[]{:S(2)}) async-start(bf16[8,16,8,192]{3,2,0,1:T(8,128)(2,1)} %copy.60), calls=%async_computation | async-start | bytes 1048576 | tf_op jit(solution)/shard_map/all_to_all | solution.py:52
  21.5 17.0 %copy-start.2 = (bf16[3,192,192]{2,1,0:T(8,128)(2,1)S(1)}, bf16[3,192,192]{2,1,0:T(8,128)(2,1)}, u32[]{:S(2)}) copy-start(bf16[3,192,192]{2,1,0:T(8,128)(2,1)} %param.18) | copy-start | bytes 663556
  55.7 1.5 %copy-start.4 = (bf16[768,192]{0,1:T(8,128)(2,1)S(1)}, bf16[768,192]{0,1:T(8,128)(2,1)}, u32[]{:S(2)}) copy-start(bf16[768,192]{0,1:T(8,128)(2,1)} %param.21) | copy-start | bytes 884740
where the time goes:
time: 85.3 us; the launch traced here: 84.8 us
  matrix products  27 us (32%)
  blocking collectives  18.2 us (21%)
  waiting for transfers between devices  14.2 us (17%)
  other arithmetic  10.9 us (13%)
  starting transfers between devices  7.39 us (9%)
  local copies, waits for them, and re-layouts  6.39 us (7%)
    all_to_all x1, blocking collectives, body(): lax.all_to_all(updated.reshape(total_rows, 1, members, model_width).astyp...  18.2 us
    all_to_all x1, waiting for transfers between devices, body(): lax.all_to_all(cells_mid.reshape(row_dev, devices_row, feat_dev, model_wi...  14.2 us
    dot_general x1, matrix products, body(): jnp.dot(hidden, mlp_out, preferred_element_type=jnp.float32)  7.68 us
    all_to_all x1, starting transfers between devices, body(): lax.all_to_all(cells_mid.reshape(row_dev, devices_row, feat_dev, model_wi...  7.39 us
    dot_general x8, matrix products, query_group(): jnp.einsum('qhd,shd->hqs', chosen, keys, precision=highest) * scale  6.36 us
    lt x8, other arithmetic, body(): key_live = lax.iota(jnp.int32, total_rows) < n_train[0]  5.22 us
    dot_general x1, matrix products, body(): jnp.einsum('rfhd,rghd->rhfg', triplet[0], triplet[1], precision=highest)  5.09 us
    sub x9, other arithmetic, softmax_rows(): exponent = jnp.exp(scores - largest)  2.01 us
  transfers between devices with their start and end apart: 1, of which 1 were waited for; matrix products, arithmetic and copies ran while one was open for 0% of the time, Pallas kernels for 0%

commit v1 on v0

--- a/solution.py
+++ b/solution.py
@@ -1,11 +1,16 @@
+import functools
 import math
 
 import jax
 import jax.numpy as jnp
 from jax import lax
+from jax.experimental import pallas as pl
+from jax.experimental.pallas import tpu as pltpu
 from jax.sharding import PartitionSpec as P
 
 HEADS = 6
+LANES = 128
+SUBLANES = 8
 
 
 norm_floor = 0.25
@@ -25,7 +30,7 @@
     return exponent / jnp.sum(exponent, axis=-1, keepdims=True)
 
 
-def body(
+def plain_body(
     cells, n_train, present, norm_gain, feat_qkv, feat_out, item_qkv, item_out, mlp_in, mlp_out
 ):
     row_dev, feature_count, model_width = cells.shape
@@ -95,6 +100,238 @@
     return returned.reshape(row_dev, feature_count, model_width)
 
 
+def matmul(left, right, dims=(1, 0)):
+    return lax.dot_general(
+        left, right, (((dims[0],), (dims[1],)), ((), ())), preferred_element_type=jnp.float32
+    )
+
+
+def identity(size):
+    down = lax.broadcasted_iota(jnp.int32, (size, size), 0)
+    across = lax.broadcasted_iota(jnp.int32, (size, size), 1)
+    return jnp.where(down == across, 1.0, 0.0).astype(jnp.bfloat16)
+
+
+def prepare_weights(qkv_ref, turned_ref, spread_ref):
+    width = qkv_ref.shape[1]
+    head = width // HEADS
+    eye = identity(width)
+    turned_ref[:width, :] = matmul(eye, qkv_ref[0], (1, 1)).astype(jnp.bfloat16)
+    turned_ref[width:, :] = matmul(eye, qkv_ref[2], (1, 1)).astype(jnp.bfloat16)
+    down = lax.broadcasted_iota(jnp.int32, (width, 4 * width), 0)
+    across = lax.broadcasted_iota(jnp.int32, (width, 4 * width), 1)
+    source = (across // (4 * head)) * head + across % head
+    pick = jnp.where(down == source, 1.0, 0.0).astype(jnp.bfloat16)
+    spread_ref[...] = matmul(qkv_ref[1], pick).astype(jnp.bfloat16)
+
+
+def attention(normed, turned_ref, spread_ref, bias_ref):
+    tokens, width = normed.shape
+    size = bias_ref.shape[0]
+    head = width // HEADS
+    wide = 4 * head
+    turned = matmul(turned_ref[...], normed, (1, 1))
+    keys = matmul(normed, spread_ref[...])
+    queries = turned[:width] * (math.log2(math.e) / math.sqrt(head))
+    query_high = queries.astype(jnp.bfloat16)
+    query_low = (queries - query_high.astype(jnp.float32)).astype(jnp.bfloat16)
+    values = turned[width:].astype(jnp.bfloat16)
+    lane = lax.broadcasted_iota(jnp.int32, (1, 4 * width), 1)
+    rounded = keys.astype(jnp.bfloat16).astype(jnp.float32)
+    keys = jnp.where(lane % wide < 2 * head, keys, keys - rounded).astype(jnp.bfloat16)
+    blocks = []
+    for block in range(tokens // size):
+        here = slice(block * size, (block + 1) * size)
+        contexts = []
+        for h in range(HEADS):
+            rows = slice(h * head, (h + 1) * head)
+            high, low = query_high[rows, here], query_low[rows, here]
+            query = jnp.concatenate([high, low, high, low], axis=0)
+            scores = matmul(keys[here, h * wide : (h + 1) * wide], query) + bias_ref[...]
+            exponent = jnp.exp2(scores - jnp.max(scores, axis=0, keepdims=True))
+            share = 1.0 / jnp.sum(exponent, axis=0, keepdims=True)
+            weights = (exponent * share).astype(jnp.bfloat16)
+            contexts.append(matmul(values[rows, here], weights))
+        blocks.append(jnp.concatenate(contexts, axis=0))
+    return blocks
+
+
+def kernel(
+    devices,
+    n_train_ref, cells_ref, present_ref, gain_ref, feat_qkv_ref, feat_out_ref, item_qkv_ref,
+    item_out_ref, mlp_in_ref, mlp_out_ref,
+    out_ref,
+    turned_f, spread_f, turned_i, spread_i, bias_f, bias_i, mid_a, mid_b, mid, send, recv, back,
+    home, send_sem, recv_sem, back_sem, home_sem,
+):
+    me = lax.axis_index("row")
+    rows, feats, width = cells_ref.shape
+    feat_dev = feats // devices
+    pairs = feat_dev // 2
+    total_rows = rows * devices
+    block = 2 * rows
+    group = devices * block
+    rest = width - LANES
+
+    barrier = pltpu.get_barrier_semaphore()
+
+    def greet(step, carry):
+        pl.semaphore_signal(
+            barrier, inc=1, device_id={"row": lax.rem(me + step, devices)},
+            device_id_type=pl.DeviceIdType.MESH,
+        )
+        return carry
+
+    lax.fori_loop(1, devices, greet, 0)
+
+    prepare_weights(feat_qkv_ref, turned_f, spread_f)
+    prepare_weights(item_qkv_ref, turned_i, spread_i)
+    live = jnp.where(present_ref[...] > 0, 0.0, masked_score)
+    bias_f[...] = jnp.broadcast_to(live, (feats, feats)).T
+    number = lax.broadcasted_iota(jnp.int32, (total_rows, total_rows), 0)
+    bias_i[...] = jnp.where(number < n_train_ref[0], 0.0, masked_score)
+
+    def feature_rows(step, carry):
+        cells = cells_ref[pl.ds(step * 2, 2)].reshape(2 * feats, width)
+        normed = layer_norm(cells, gain_ref[0:1, :]).astype(jnp.bfloat16)
+        contexts = attention(normed, turned_f, spread_f, bias_f)
+        context = jnp.concatenate(contexts, axis=1).astype(jnp.bfloat16)
+        updated = cells + matmul(context, feat_out_ref[...], (0, 0))
+        here = pl.ds(pl.multiple_of(step * 2 * feats, 2 * feats), 2 * feats)
+        mid_a[here, :] = updated[:, :LANES]
+        mid_b[here, :rest] = updated[:, LANES:]
+        return carry
+
+    lax.fori_loop(0, rows // 2, feature_rows, 0)
+
+    def outgoing(pair, step):
+        to = lax.rem(me + step, devices)
+        return pltpu.make_async_remote_copy(
+            src_ref=send.at[pair, to], dst_ref=recv.at[pair, me],
+            send_sem=send_sem.at[pair, step], recv_sem=recv_sem.at[pair, step],
+            device_id={"row": to}, device_id_type=pl.DeviceIdType.MESH,
+        )
+
+    def returning(pair, step):
+        to = lax.rem(me + step, devices)
+        return pltpu.make_async_remote_copy(
+            src_ref=back.at[pair, to], dst_ref=home.at[pair, me],
+            send_sem=back_sem.at[pair, step], recv_sem=home_sem.at[pair, step],
+            device_id={"row": to}, device_id_type=pl.DeviceIdType.MESH,
+        )
+
+    def each(act):
+        def one(step, carry):
+            act(step)
+            return carry
+
+        lax.fori_loop(1, devices, one, 0)
+
+    pl.semaphore_wait(barrier, devices - 1)
+
+    for pair in range(pairs):
+        firsts, lasts = [], []
+        for owner in range(devices):
+            for one in range(2):
+                take = pl.ds(owner * feat_dev + pair * 2 + one, rows, stride=feats)
+                firsts.append(mid_a[take, :])
+                lasts.append(mid_b[take, :])
+        stream = jnp.concatenate(
+            [jnp.concatenate(firsts, axis=0), jnp.concatenate(lasts, axis=0)[:, :rest]], axis=1
+        )
+        mid[pair] = stream
+        normed = layer_norm(stream, gain_ref[1:2, :]).astype(jnp.bfloat16)
+        send[pair] = normed.reshape(devices, block, width)
+        recv[pair, me] = send[pair, me]
+        each(lambda step: outgoing(pair, step).start())
+
+    def item_pair(pair, carry):
+        each(lambda step: outgoing(pair, step).wait_recv())
+        arrived = recv[pair].astype(jnp.float32).reshape(devices, 2, rows, width)
+        normed = jnp.concatenate(
+            [arrived[:, one].reshape(total_rows, width) for one in range(2)], axis=0
+        ).astype(jnp.bfloat16)
+        contexts = attention(normed, turned_i, spread_i, bias_i)
+        turned = [context.T.reshape(devices, 1, rows, width) for context in contexts]
+        context = jnp.concatenate(turned, axis=1).reshape(devices, block, width)
+        back[pair] = context.astype(jnp.bfloat16)
+        home[pair, me] = back[pair, me]
+        each(lambda step: returning(pair, step).start())
+        return carry
+
+    lax.fori_loop(0, pairs, item_pair, 0)
+
+    def finish(pair, carry):
+        each(lambda step: returning(pair, step).wait_recv())
+        context = home[pair].reshape(group, width)
+        late = mid[pair] + matmul(context, item_out_ref[...])
+        normed = layer_norm(late, gain_ref[2:3, :]).astype(jnp.bfloat16)
+        inner = matmul(normed, mlp_in_ref[...])
+        hidden = (0.5 * inner * (1.0 + lax.erf(inner * math.sqrt(0.5)))).astype(jnp.bfloat16)
+        done = late + matmul(hidden, mlp_out_ref[...])
+        for owner in range(devices):
+            for one in range(2):
+                start = (owner * 2 + one) * rows
+                put = pl.ds(owner * feat_dev + pair * 2 + one, rows, stride=feats)
+                mid_a[put, :] = done[start : start + rows, :LANES]
+                mid_b[put, :rest] = done[start : start + rows, LANES:]
+        return carry
+
+    lax.fori_loop(0, pairs, finish, 0)
+    for row in range(rows):
+        out_ref[row, :, :LANES] = mid_a[row * feats : (row + 1) * feats, :]
+        out_ref[row, :, LANES:] = mid_b[row * feats : (row + 1) * feats, :rest]
+
+    for pair in range(pairs):
+        each(lambda step: outgoing(pair, step).wait_send())
+        each(lambda step: returning(pair, step).wait_send())
+
+
+def body(
+    cells, n_train, present, norm_gain, feat_qkv, feat_out, item_qkv, item_out, mlp_in, mlp_out
+):
+    devices = lax.axis_size("row")
+    rows, feats, width = cells.shape
+    feat_dev = feats // devices
+    fits = rows == SUBLANES and feat_dev % 2 == 0 and LANES < width <= 2 * LANES
+    fits = fits and rows * devices == LANES and feats == LANES and width % (HEADS * 16) == 0
+    if not fits:
+        return plain_body(
+            cells, n_train, present, norm_gain, feat_qkv, feat_out, item_qkv, item_out, mlp_in,
+            mlp_out,
+        )
+    total_rows = rows * devices
+    pairs = feat_dev // 2
+    vmem = pl.BlockSpec(memory_space=pltpu.VMEM)
+    bf16, f32 = jnp.bfloat16, jnp.float32
+    slots = pltpu.VMEM((pairs, devices, 2 * rows, width), bf16)
+    sems = pltpu.SemaphoreType.DMA((pairs, devices))
+    return pl.pallas_call(
+        functools.partial(kernel, devices),
+        out_shape=jax.ShapeDtypeStruct(cells.shape, f32),
+        in_specs=[pl.BlockSpec(memory_space=pltpu.SMEM)] + [vmem] * 9,
+        out_specs=vmem,
+        scratch_shapes=[
+            pltpu.VMEM((2 * width, width), bf16),
+            pltpu.VMEM((width, 4 * width), bf16),
+            pltpu.VMEM((2 * width, width), bf16),
+            pltpu.VMEM((width, 4 * width), bf16),
+            pltpu.VMEM((feats, feats), f32),
+            pltpu.VMEM((total_rows, total_rows), f32),
+            pltpu.VMEM((rows * feats, LANES), f32),
+            pltpu.VMEM((rows * feats, LANES), f32),
+            pltpu.VMEM((pairs, 2 * total_rows, width), f32),
+            slots, slots, slots, slots, sems, sems, sems, sems,
+        ],
+        compiler_params=pltpu.CompilerParams(
+            collective_id=0, has_side_effects=True, vmem_limit_bytes=48 * 1024 * 1024
+        ),
+    )(
+        n_train, cells, present.reshape(1, feats), norm_gain, feat_qkv, feat_out, item_qkv, item_out,
+        mlp_in, mlp_out,
+    )
+
+
 def solution(mesh):
     return jax.shard_map(
         body,

time: 85.3 us -> 44 us (0.52)
  Pallas kernels: 0 us -> 38.2 us
  matrix products: 27 us -> 0 us
  blocking collectives: 18.2 us -> 0 us
  waiting for transfers between devices: 14.2 us -> 0 us
  other arithmetic: 10.9 us -> 0 us
  starting transfers between devices: 7.39 us -> 0 us
  local copies, waits for them, and re-layouts: 6.39 us -> 4.81 us
    pallas_call x0 -> x1, Pallas kernels: none -> 38.2 us  [body(): pl.pallas_call(functools.partial(kernel, devices), out_shape=jax.ShapeDty...]
    dot_general x24 -> x0, matrix products: 27 us -> none  [the longest x1 7.68 us: body(): jnp.dot(hidden, mlp_out, preferred_element_type=jnp.float32)]
    all_to_all x1 -> x0, blocking collectives: 18.2 us -> none  [body(): lax.all_to_all(updated.reshape(total_rows, 1, members, model_width).astyp...]
    all_to_all x1 -> x0, waiting for transfers between devices: 14.2 us -> none  [body(): lax.all_to_all(cells_mid.reshape(row_dev, devices_row, feat_dev, model_wi...]
    all_to_all x1 -> x0, starting transfers between devices: 7.39 us -> none  [body(): lax.all_to_all(cells_mid.reshape(row_dev, devices_row, feat_dev, model_wi...]
    lt x8 -> x0, other arithmetic: 5.22 us -> none  [body(): key_live = lax.iota(jnp.int32, total_rows) < n_train[0]]
    convert_element_type x5 -> x0, local copies, waits for them, and re-layouts: 3.98 us -> none  [the longest x1 1.31 us: body(): arrived = lax.all_to_all(cells_mid.reshape(row_dev, devices_row, feat_dev...]
    reduce_sum x5 -> x0, other arithmetic: 3.09 us -> none  [the longest x3 1.71 us: layer_norm(): spread = jnp.mean(centred * centred, axis=-1, keepdims=True)]
  transfers between devices with their start and end apart: 1 -> 0, of which waited for: 1 -> 0; matrix products, arithmetic and copies ran while one was open for 0% -> 0% of each run, Pallas kernels for 0% -> 0%
where the time goes in v1:
time: 44 us; the launch traced here: 43.8 us
  Pallas kernels  38.2 us (87%)
  local copies, waits for them, and re-layouts  4.81 us (11%)
  between operations  0.78 us (2%)
    pallas_call x1, Pallas kernels, body(): pl.pallas_call(functools.partial(kernel, devices), out_shape=jax.ShapeDty...  38.2 us
    unnamed x16, local copies, waits for them, and re-layouts  3.59 us
    pallas_call x1, local copies, waits for them, and re-layouts, body(): pl.pallas_call(functools.partial(kernel, devices), out_shape=jax.ShapeDty...  1.22 us

profile of v1, /device:TPU:0, one launch (start us, length us, event | category | flops | bytes accessed | tf_op | source)
XLA Modules:
  0.0 43.8 jit_solution(7537744999829773852)
XLA Ops:
  0.7 1.1 %copy.12.mlp_out_ref = bf16[768,192]{1,0:T(8,128)(2,1)S(1)} copy(bf16[768,192]{0,1:T(8,128)(2,1)} %param.19) | data formatting | bytes 589824 | tf_op args[9]
  1.8 0.0 copy-start
  1.8 0.0 copy-start.1
  1.8 0.0 copy-start.2
  1.8 0.0 copy-start.3
  1.8 0.0 copy-start.5
  1.8 0.0 copy-start.6
  1.9 1.5 %copy.11.cells_ref = f32[8,128,192]{2,1,0:T(8,128)S(1)} copy(f32[8,128,192]{1,2,0:T(8,128)} %param.10) | data formatting | bytes 1572864 | tf_op args[0]
  3.4 0.0 copy-done
  3.4 0.0 copy-done.1
  3.4 0.0 copy-done.2
  3.4 0.0 copy-done.3
  3.4 0.0 copy-done.5
  3.5 0.0 copy-done.6
  3.5 0.0 copy-start.4
  3.5 0.9 %copy-done.4 = bf16[192,192]{1,0:T(8,128)(2,1)S(1)} copy-done((bf16[192,192]{1,0:T(8,128)(2,1)S(1)}, bf16[192,192]{1,0:T(8,128)(2,1)}, u32[]{:S(2)}) %copy-start.4) | copy-done | bytes 73752
  4.4 38.2 %shard_map.100 = f32[8,128,192]{2,1,0:T(8,128)S(1)} custom-call(s32[1]{0:T(128)S(6)} %copy.14.n_train_ref, f32[8,128,192]{2,1,0:T(8,128)S(1)} %copy.11.cells_ref, s32[1,128]{1,0:T(1,128)S(1)} %bitcast.1, f32[3,192]{1,0:T(4,128)S(1)} %copy-done.5, bf16[3,192,192]{2,1,0:T(8,128)(2,1)S(1)} %copy-done, bf16[192,192]{1,0:T(8,128)(2,1)S(1)} %copy-done.3, ...), custom_call_target="tpu_custom_call" | custom-call | tf_op jit(solution)/shard_map/pallas_call | solution.py:309
  42.6 1.2 %copy.13 = f32[8,128,192]{1,2,0:T(8,128)} copy(f32[8,128,192]{2,1,0:T(8,128)S(1)} %shard_map.100) | data formatting | bytes 1572864 | tf_op jit(solution)/shard_map/pallas_call | solution.py:309
Async XLA Ops:
  1.8 1.6 %copy-start = (bf16[3,192,192]{2,1,0:T(8,128)(2,1)S(1)}, bf16[3,192,192]{2,1,0:T(8,128)(2,1)}, u32[]{:S(2)}) copy-start(bf16[3,192,192]{2,1,0:T(8,128)(2,1)} %feat_qkv_ref.1) | copy-start | bytes 663556
  1.8 1.6 %copy-start.1 = (bf16[3,192,192]{2,1,0:T(8,128)(2,1)S(1)}, bf16[3,192,192]{2,1,0:T(8,128)(2,1)}, u32[]{:S(2)}) copy-start(bf16[3,192,192]{2,1,0:T(8,128)(2,1)} %item_qkv_ref.1) | copy-start | bytes 663556
  1.8 1.6 %copy-start.2 = (bf16[192,768]{1,0:T(8,128)(2,1)S(1)}, bf16[192,768]{1,0:T(8,128)(2,1)}, u32[]{:S(2)}) copy-start(bf16[192,768]{1,0:T(8,128)(2,1)} %mlp_in_ref.1) | copy-start | bytes 884740
  1.8 1.6 %copy-start.3 = (bf16[192,192]{1,0:T(8,128)(2,1)S(1)}, bf16[192,192]{1,0:T(8,128)(2,1)}, u32[]{:S(2)}) copy-start(bf16[192,192]{1,0:T(8,128)(2,1)} %feat_out_ref.1) | copy-start | bytes 221188
  1.8 1.6 %copy-start.5 = (f32[3,192]{1,0:T(4,128)S(1)}, f32[3,192]{1,0:T(4,128)}, u32[]{:S(2)}) copy-start(f32[3,192]{1,0:T(4,128)} %gain_ref.1) | copy-start | bytes 6916
  1.8 1.6 %copy-start.6 = (s32[128]{0:T(128)S(1)}, s32[128]{0:T(128)}, u32[]{:S(2)}) copy-start(s32[128]{0:T(128)} %param.12) | copy-start | bytes 1540
  3.5 0.9 %copy-start.4 = (bf16[192,192]{1,0:T(8,128)(2,1)S(1)}, bf16[192,192]{1,0:T(8,128)(2,1)}, u32[]{:S(2)}) copy-start(bf16[192,192]{1,0:T(8,128)(2,1)} %item_out_ref.1) | copy-start | bytes 221188

commit v2 on v1

--- a/solution.py
+++ b/solution.py
@@ -172,6 +172,23 @@
     block = 2 * rows
     group = devices * block
     rest = width - LANES
+    quarter = devices // 4
+    order = list(range(2 * quarter, devices)) + list(range(quarter, 2 * quarter))
+    order += list(range(1, quarter))
+
+    def pack(slots, pair, tokens):
+        last = tokens[:, LANES:].reshape(devices, 2, rows, rest)
+        last = jnp.concatenate([last[:, 0], last[:, 1]], axis=-1)
+        slots[pair, :, :block] = tokens[:, :LANES].reshape(devices, block, LANES).astype(jnp.bfloat16)
+        slots[pair, :, block:] = last.astype(jnp.bfloat16)
+
+    def unpack(slots, pair):
+        first = slots[pair, :, :block].astype(jnp.float32).reshape(devices, 2, rows, LANES)
+        last = slots[pair, :, block:].astype(jnp.float32)
+        last = jnp.concatenate(
+            [last[:, None, :, one * rest : (one + 1) * rest] for one in range(2)], axis=1
+        )
+        return jnp.concatenate([first, last], axis=-1)
 
     barrier = pltpu.get_barrier_semaphore()
 
@@ -240,35 +257,40 @@
             [jnp.concatenate(firsts, axis=0), jnp.concatenate(lasts, axis=0)[:, :rest]], axis=1
         )
         mid[pair] = stream
-        normed = layer_norm(stream, gain_ref[1:2, :]).astype(jnp.bfloat16)
-        send[pair] = normed.reshape(devices, block, width)
+        normed = layer_norm(stream, gain_ref[1:2, :])
+        pack(send, pair, normed)
         recv[pair, me] = send[pair, me]
-        each(lambda step: outgoing(pair, step).start())
+        for step in order:
+            outgoing(pair, step).start()
 
     def item_pair(pair, carry):
         each(lambda step: outgoing(pair, step).wait_recv())
-        arrived = recv[pair].astype(jnp.float32).reshape(devices, 2, rows, width)
+        arrived = unpack(recv, pair)
         normed = jnp.concatenate(
             [arrived[:, one].reshape(total_rows, width) for one in range(2)], axis=0
         ).astype(jnp.bfloat16)
         contexts = attention(normed, turned_i, spread_i, bias_i)
-        turned = [context.T.reshape(devices, 1, rows, width) for context in contexts]
-        context = jnp.concatenate(turned, axis=1).reshape(devices, block, width)
-        back[pair] = context.astype(jnp.bfloat16)
+        first = jnp.concatenate(
+            [c[:LANES].T.reshape(devices, 1, rows, LANES) for c in contexts], axis=1
+        )
+        last = jnp.concatenate([c[LANES:] for c in contexts], axis=0).T
+        back[pair, :, :block] = first.reshape(devices, block, LANES).astype(jnp.bfloat16)
+        back[pair, :, block:] = last.reshape(devices, rows, LANES).astype(jnp.bfloat16)
         home[pair, me] = back[pair, me]
-        each(lambda step: returning(pair, step).start())
+        for step in order:
+            returning(pair, step).start()
         return carry
 
     lax.fori_loop(0, pairs, item_pair, 0)
 
     def finish(pair, carry):
         each(lambda step: returning(pair, step).wait_recv())
-        context = home[pair].reshape(group, width)
+        context = unpack(home, pair).reshape(group, width).astype(jnp.bfloat16)
         late = mid[pair] + matmul(context, item_out_ref[...])
         normed = layer_norm(late, gain_ref[2:3, :]).astype(jnp.bfloat16)
         inner = matmul(normed, mlp_in_ref[...])
         hidden = (0.5 * inner * (1.0 + lax.erf(inner * math.sqrt(0.5)))).astype(jnp.bfloat16)
-        done = late + matmul(hidden, mlp_out_ref[...])
+        done = late + matmul(hidden, mlp_out_ref[...], (1, 1))
         for owner in range(devices):
             for one in range(2):
                 start = (owner * 2 + one) * rows
@@ -293,7 +315,7 @@
     devices = lax.axis_size("row")
     rows, feats, width = cells.shape
     feat_dev = feats // devices
-    fits = rows == SUBLANES and feat_dev % 2 == 0 and LANES < width <= 2 * LANES
+    fits = rows == SUBLANES and devices % 4 == 0 and feat_dev % 2 == 0 and 2 * width == 3 * LANES
     fits = fits and rows * devices == LANES and feats == LANES and width % (HEADS * 16) == 0
     if not fits:
         return plain_body(
@@ -304,7 +326,7 @@
     pairs = feat_dev // 2
     vmem = pl.BlockSpec(memory_space=pltpu.VMEM)
     bf16, f32 = jnp.bfloat16, jnp.float32
-    slots = pltpu.VMEM((pairs, devices, 2 * rows, width), bf16)
+    slots = pltpu.VMEM((pairs, devices, 3 * rows, LANES), bf16)
     sems = pltpu.SemaphoreType.DMA((pairs, devices))
     return pl.pallas_call(
         functools.partial(kernel, devices),
@@ -328,7 +350,7 @@
         ),
     )(
         n_train, cells, present.reshape(1, feats), norm_gain, feat_qkv, feat_out, item_qkv, item_out,
-        mlp_in, mlp_out,
+        mlp_in, mlp_out.T,
     )
 
 

time: 44 us -> 38.1 us (0.87)
  Pallas kernels: 38.2 us -> 34.4 us
  local copies, waits for them, and re-layouts: 4.81 us -> 2.81 us
    pallas_call x1, Pallas kernels: 38.2 us -> 34.4 us  [body(): pl.pallas_call(functools.partial(kernel, devices), out_shape=jax.ShapeDty...]
    unnamed x16 -> x17, local copies, waits for them, and re-layouts: 3.59 us -> 1.59 us
where the time goes in v2:
time: 38.1 us; the launch traced here: 38 us
  Pallas kernels  34.4 us (90%)
  local copies, waits for them, and re-layouts  2.81 us (7%)
  between operations  0.79 us (2%)
    pallas_call x1, Pallas kernels, body(): pl.pallas_call(functools.partial(kernel, devices), out_shape=jax.ShapeDty...  34.4 us
    unnamed x17, local copies, waits for them, and re-layouts  1.59 us
    pallas_call x1, local copies, waits for them, and re-layouts, body(): pl.pallas_call(functools.partial(kernel, devices), out_shape=jax.ShapeDty...  1.22 us

profile of v2, /device:TPU:0, one launch (start us, length us, event | category | flops | bytes accessed | tf_op | source)
XLA Modules:
  0.0 38.0 jit_solution(3913839274412602575)
XLA Ops:
  0.7 0.0 copy-start
  0.7 0.0 copy-start.1
  0.7 0.0 copy-start.2
  0.7 0.0 copy-start.3
  0.7 0.0 copy-start.4
  0.7 0.0 copy-start.5
  0.7 0.0 copy-start.6
  0.7 0.0 copy-start.7
  0.7 1.6 %copy.11.cells_ref = f32[8,128,192]{2,1,0:T(8,128)S(1)} copy(f32[8,128,192]{1,2,0:T(8,128)} %param.10) | data formatting | bytes 1572864 | tf_op args[0]
  2.3 0.0 copy-done
  2.3 0.0 copy-done.1
  2.3 0.0 copy-done.2
  2.3 0.0 copy-done.3
  2.3 0.0 copy-done.4
  2.3 0.0 copy-done.5
  2.4 0.0 copy-done.6
  2.4 0.0 copy-done.7
  2.4 34.4 %shard_map.100 = f32[8,128,192]{2,1,0:T(8,128)S(1)} custom-call(s32[1]{0:T(128)S(6)} %copy.13.n_train_ref, f32[8,128,192]{2,1,0:T(8,128)S(1)} %copy.11.cells_ref, s32[1,128]{1,0:T(1,128)S(1)} %bitcast.3, f32[3,192]{1,0:T(4,128)S(1)} %copy-done.6, bf16[3,192,192]{2,1,0:T(8,128)(2,1)S(1)} %copy-done, bf16[192,192]{1,0:T(8,128)(2,1)S(1)} %copy-done.4, ...), custom_call_target="tpu_custom_call" | custom-call | tf_op jit(solution)/shard_map/pallas_call | solution.py:331
  36.7 1.2 %copy.12 = f32[8,128,192]{1,2,0:T(8,128)} copy(f32[8,128,192]{2,1,0:T(8,128)S(1)} %shard_map.100) | data formatting | bytes 1572864 | tf_op jit(solution)/shard_map/pallas_call | solution.py:331
Async XLA Ops:
  0.7 1.6 %copy-start = (bf16[3,192,192]{2,1,0:T(8,128)(2,1)S(1)}, bf16[3,192,192]{2,1,0:T(8,128)(2,1)}, u32[]{:S(2)}) copy-start(bf16[3,192,192]{2,1,0:T(8,128)(2,1)} %feat_qkv_ref.1) | copy-start | bytes 663556
  0.7 1.6 %copy-start.1 = (bf16[3,192,192]{2,1,0:T(8,128)(2,1)S(1)}, bf16[3,192,192]{2,1,0:T(8,128)(2,1)}, u32[]{:S(2)}) copy-start(bf16[3,192,192]{2,1,0:T(8,128)(2,1)} %item_qkv_ref.1) | copy-start | bytes 663556
  0.7 1.6 %copy-start.2 = (bf16[192,768]{1,0:T(8,128)(2,1)S(1)}, bf16[192,768]{1,0:T(8,128)(2,1)}, u32[]{:S(2)}) copy-start(bf16[192,768]{1,0:T(8,128)(2,1)} %mlp_in_ref.1) | copy-start | bytes 884740
  0.7 1.6 %copy-start.3 = (bf16[768,192]{0,1:T(8,128)(2,1)S(1)}, bf16[768,192]{0,1:T(8,128)(2,1)}, u32[]{:S(2)}) copy-start(bf16[768,192]{0,1:T(8,128)(2,1)} %param.19) | copy-start | bytes 884740
  0.7 1.6 %copy-start.4 = (bf16[192,192]{1,0:T(8,128)(2,1)S(1)}, bf16[192,192]{1,0:T(8,128)(2,1)}, u32[]{:S(2)}) copy-start(bf16[192,192]{1,0:T(8,128)(2,1)} %feat_out_ref.1) | copy-start | bytes 221188
  0.7 1.6 %copy-start.5 = (bf16[192,192]{1,0:T(8,128)(2,1)S(1)}, bf16[192,192]{1,0:T(8,128)(2,1)}, u32[]{:S(2)}) copy-start(bf16[192,192]{1,0:T(8,128)(2,1)} %item_out_ref.1) | copy-start | bytes 221188
  0.7 1.6 %copy-start.6 = (f32[3,192]{1,0:T(4,128)S(1)}, f32[3,192]{1,0:T(4,128)}, u32[]{:S(2)}) copy-start(f32[3,192]{1,0:T(4,128)} %gain_ref.1) | copy-start | bytes 6916
  0.7 1.6 %copy-start.7 = (s32[128]{0:T(128)S(1)}, s32[128]{0:T(128)}, u32[]{:S(2)}) copy-start(s32[128]{0:T(128)} %param.12) | copy-start | bytes 1540

commit v3 on v2

--- a/solution.py
+++ b/solution.py
@@ -165,16 +165,14 @@
     home, send_sem, recv_sem, back_sem, home_sem,
 ):
     me = lax.axis_index("row")
-    rows, feats, width = cells_ref.shape
+    rows, width, feats = cells_ref.shape
     feat_dev = feats // devices
     pairs = feat_dev // 2
     total_rows = rows * devices
     block = 2 * rows
     group = devices * block
     rest = width - LANES
-    quarter = devices // 4
-    order = list(range(2 * quarter, devices)) + list(range(quarter, 2 * quarter))
-    order += list(range(1, quarter))
+    order = range(1, devices)
 
     def pack(slots, pair, tokens):
         last = tokens[:, LANES:].reshape(devices, 2, rows, rest)
@@ -209,7 +207,7 @@
     bias_i[...] = jnp.where(number < n_train_ref[0], 0.0, masked_score)
 
     def feature_rows(step, carry):
-        cells = cells_ref[pl.ds(step * 2, 2)].reshape(2 * feats, width)
+        cells = jnp.concatenate([cells_ref[step * 2 + one].T for one in range(2)], axis=0)
         normed = layer_norm(cells, gain_ref[0:1, :]).astype(jnp.bfloat16)
         contexts = attention(normed, turned_f, spread_f, bias_f)
         context = jnp.concatenate(contexts, axis=1).astype(jnp.bfloat16)
@@ -315,7 +313,7 @@
     devices = lax.axis_size("row")
     rows, feats, width = cells.shape
     feat_dev = feats // devices
-    fits = rows == SUBLANES and devices % 4 == 0 and feat_dev % 2 == 0 and 2 * width == 3 * LANES
+    fits = rows == SUBLANES and feat_dev % 2 == 0 and 2 * width == 3 * LANES
     fits = fits and rows * devices == LANES and feats == LANES and width % (HEADS * 16) == 0
     if not fits:
         return plain_body(
@@ -349,7 +347,7 @@
             collective_id=0, has_side_effects=True, vmem_limit_bytes=48 * 1024 * 1024
         ),
     )(
-        n_train, cells, present.reshape(1, feats), norm_gain, feat_qkv, feat_out, item_qkv, item_out,
+        n_train, jnp.transpose(cells, (0, 2, 1)), present.reshape(1, feats), norm_gain, feat_qkv, feat_out, item_qkv, item_out,
         mlp_in, mlp_out.T,
     )
 

time: 38.1 us -> 43.6 us (1.14)
  local copies, waits for them, and re-layouts: 2.81 us -> 8.63 us
  Pallas kernels: 34.4 us -> 33.9 us
    unnamed x17 -> x18, local copies, waits for them, and re-layouts: 1.59 us -> 7.41 us
    pallas_call x1, Pallas kernels: 34.4 us -> 33.9 us  [body(): pl.pallas_call(functools.partial(kernel, devices), out_shape=jax.ShapeDty...]
where the time goes in v3:
time: 43.6 us; the launch traced here: 43.2 us
  Pallas kernels  33.9 us (78%)
  local copies, waits for them, and re-layouts  8.63 us (20%)
  between operations  0.69 us (2%)
    pallas_call x1, Pallas kernels, body(): pl.pallas_call(functools.partial(kernel, devices), out_shape=jax.ShapeDty...  33.9 us
    unnamed x18, local copies, waits for them, and re-layouts  7.41 us
    pallas_call x1, local copies, waits for them, and re-layouts, body(): pl.pallas_call(functools.partial(kernel, devices), out_shape=jax.ShapeDty...  1.22 us

profile of v3, /device:TPU:0, one launch (start us, length us, event | category | flops | bytes accessed | tf_op | source)
XLA Modules:
  0.0 43.2 jit_solution(11085666315525569936)
XLA Ops:
  0.0 0.0 copy-start.7
  0.7 0.0 copy-start.8
  0.7 0.0 copy-done.7
  0.7 0.6 %copy-done.8 = s32[128]{0:T(128)S(1)} copy-done((s32[128]{0:T(128)S(1)}, s32[128]{0:T(128)}, u32[]{:S(2)}) %copy-start.8) | copy-done | bytes 536
  1.3 0.0 copy-start
  1.3 1.1 %copy-done = f32[8,128,192]{1,2,0:T(8,128)S(1)} copy-done((f32[8,128,192]{1,2,0:T(8,128)S(1)}, f32[8,128,192]{1,2,0:T(8,128)}, u32[]{:S(2)}) %copy-start) | copy-done | bytes 786456
  2.5 0.0 copy-start.1
  2.5 1.0 %copy-done.1 = bf16[3,192,192]{2,1,0:T(8,128)(2,1)S(1)} copy-done((bf16[3,192,192]{2,1,0:T(8,128)(2,1)S(1)}, bf16[3,192,192]{2,1,0:T(8,128)(2,1)}, u32[]{:S(2)}) %copy-start.1) | copy-done | bytes 221208
  3.4 0.0 copy-start.2
  3.4 1.0 %copy-done.2 = bf16[3,192,192]{2,1,0:T(8,128)(2,1)S(1)} copy-done((bf16[3,192,192]{2,1,0:T(8,128)(2,1)S(1)}, bf16[3,192,192]{2,1,0:T(8,128)(2,1)}, u32[]{:S(2)}) %copy-start.2) | copy-done | bytes 221208
  4.4 0.0 copy-start.3
  4.4 1.0 %copy-done.3 = bf16[192,768]{1,0:T(8,128)(2,1)S(1)} copy-done((bf16[192,768]{1,0:T(8,128)(2,1)S(1)}, bf16[192,768]{1,0:T(8,128)(2,1)}, u32[]{:S(2)}) %copy-start.3) | copy-done | bytes 294936
  5.3 0.0 copy-start.4
  5.3 1.0 %copy-done.4 = bf16[768,192]{0,1:T(8,128)(2,1)S(1)} copy-done((bf16[768,192]{0,1:T(8,128)(2,1)S(1)}, bf16[768,192]{0,1:T(8,128)(2,1)}, u32[]{:S(2)}) %copy-start.4) | copy-done | bytes 294936
  6.3 0.0 copy-start.5
  6.3 0.9 %copy-done.5 = bf16[192,192]{1,0:T(8,128)(2,1)S(1)} copy-done((bf16[192,192]{1,0:T(8,128)(2,1)S(1)}, bf16[192,192]{1,0:T(8,128)(2,1)}, u32[]{:S(2)}) %copy-start.5) | copy-done | bytes 73752
  7.2 0.0 copy-start.6
  7.2 0.9 %copy-done.6 = bf16[192,192]{1,0:T(8,128)(2,1)S(1)} copy-done((bf16[192,192]{1,0:T(8,128)(2,1)S(1)}, bf16[192,192]{1,0:T(8,128)(2,1)}, u32[]{:S(2)}) %copy-start.6) | copy-done | bytes 73752
  8.1 33.9 %shard_map.100 = f32[8,128,192]{2,1,0:T(8,128)S(1)} custom-call(s32[1]{0:T(128)S(6)} %copy.12.n_train_ref, f32[8,192,128]{2,1,0:T(8,128)S(1)} %bitcast.3, s32[1,128]{1,0:T(1,128)S(1)} %bitcast.5, f32[3,192]{1,0:T(4,128)S(1)} %copy-done.7, bf16[3,192,192]{2,1,0:T(8,128)(2,1)S(1)} %copy-done.1, bf16[192,192]{1,0:T(8,128)(2,1)S(1)} %copy-done.5, ...), custom_call_target="tpu_custom_call" | custom-call | tf_op jit(solution)/shard_map/pallas_call | solution.py:329
  42.0 1.2 %copy.11 = f32[8,128,192]{1,2,0:T(8,128)} copy(f32[8,128,192]{2,1,0:T(8,128)S(1)} %shard_map.100) | data formatting | bytes 1572864 | tf_op jit(solution)/shard_map/pallas_call | solution.py:329
Async XLA Ops:
  0.0 0.7 %copy-start.7 = (f32[3,192]{1,0:T(4,128)S(1)}, f32[3,192]{1,0:T(4,128)}, u32[]{:S(2)}) copy-start(f32[3,192]{1,0:T(4,128)} %gain_ref.1) | copy-start | bytes 6916
  0.7 0.7 %copy-start.8 = (s32[128]{0:T(128)S(1)}, s32[128]{0:T(128)}, u32[]{:S(2)}) copy-start(s32[128]{0:T(128)} %param.12) | copy-start | bytes 1540
  1.3 1.1 %copy-start = (f32[8,128,192]{1,2,0:T(8,128)S(1)}, f32[8,128,192]{1,2,0:T(8,128)}, u32[]{:S(2)}) copy-start(f32[8,128,192]{1,2,0:T(8,128)} %param.10) | copy-start | bytes 2359300
  2.5 1.0 %copy-start.1 = (bf16[3,192,192]{2,1,0:T(8,128)(2,1)S(1)}, bf16[3,192,192]{2,1,0:T(8,128)(2,1)}, u32[]{:S(2)}) copy-start(bf16[3,192,192]{2,1,0:T(8,128)(2,1)} %feat_qkv_ref.1) | copy-start | bytes 663556
  3.4 1.0 %copy-start.2 = (bf16[3,192,192]{2,1,0:T(8,128)(2,1)S(1)}, bf16[3,192,192]{2,1,0:T(8,128)(2,1)}, u32[]{:S(2)}) copy-start(bf16[3,192,192]{2,1,0:T(8,128)(2,1)} %item_qkv_ref.1) | copy-start | bytes 663556
  4.4 1.0 %copy-start.3 = (bf16[192,768]{1,0:T(8,128)(2,1)S(1)}, bf16[192,768]{1,0:T(8,128)(2,1)}, u32[]{:S(2)}) copy-start(bf16[192,768]{1,0:T(8,128)(2,1)} %mlp_in_ref.1) | copy-start | bytes 884740
  5.3 1.0 %copy-start.4 = (bf16[768,192]{0,1:T(8,128)(2,1)S(1)}, bf16[768,192]{0,1:T(8,128)(2,1)}, u32[]{:S(2)}) copy-start(bf16[768,192]{0,1:T(8,128)(2,1)} %param.19) | copy-start | bytes 884740
  6.3 0.9 %copy-start.5 = (bf16[192,192]{1,0:T(8,128)(2,1)S(1)}, bf16[192,192]{1,0:T(8,128)(2,1)}, u32[]{:S(2)}) copy-start(bf16[192,192]{1,0:T(8,128)(2,1)} %feat_out_ref.1) | copy-start | bytes 221188
  7.2 0.9 %copy-start.6 = (bf16[192,192]{1,0:T(8,128)(2,1)S(1)}, bf16[192,192]{1,0:T(8,128)(2,1)}, u32[]{:S(2)}) copy-start(bf16[192,192]{1,0:T(8,128)(2,1)} %item_out_ref.1) | copy-start | bytes 221188

commit v4 on v3

--- a/solution.py
+++ b/solution.py
@@ -158,9 +158,11 @@
 
 def kernel(
     devices,
-    n_train_ref, cells_ref, present_ref, gain_ref, feat_qkv_ref, feat_out_ref, item_qkv_ref,
-    item_out_ref, mlp_in_ref, mlp_out_ref,
+    n_train_ref, gain_ref, present_ref, feat_qkv_hbm, item_qkv_hbm, cells_hbm, feat_out_hbm,
+    item_out_hbm, mlp_in_hbm, mlp_out_hbm,
     out_ref,
+    feat_qkv_ref, item_qkv_ref, cells_ref, feat_out_ref, item_out_ref, mlp_in_ref, mlp_out_ref,
+    load_sem,
     turned_f, spread_f, turned_i, spread_i, bias_f, bias_i, mid_a, mid_b, mid, send, recv, back,
     home, send_sem, recv_sem, back_sem, home_sem,
 ):
@@ -188,6 +190,16 @@
         )
         return jnp.concatenate([first, last], axis=-1)
 
+    loads = [
+        pltpu.make_async_copy(source, target, load_sem.at[number])
+        for number, (source, target) in enumerate((
+            (feat_qkv_hbm, feat_qkv_ref), (item_qkv_hbm, item_qkv_ref), (cells_hbm, cells_ref),
+            (feat_out_hbm, feat_out_ref), (item_out_hbm, item_out_ref), (mlp_in_hbm, mlp_in_ref),
+            (mlp_out_hbm, mlp_out_ref),
+        ))
+    ]
+    for load in loads:
+        load.start()
     barrier = pltpu.get_barrier_semaphore()
 
     def greet(step, carry):
@@ -199,12 +211,17 @@
 
     lax.fori_loop(1, devices, greet, 0)
 
+    loads[0].wait()
     prepare_weights(feat_qkv_ref, turned_f, spread_f)
+    loads[1].wait()
     prepare_weights(item_qkv_ref, turned_i, spread_i)
     live = jnp.where(present_ref[...] > 0, 0.0, masked_score)
     bias_f[...] = jnp.broadcast_to(live, (feats, feats)).T
     number = lax.broadcasted_iota(jnp.int32, (total_rows, total_rows), 0)
     bias_i[...] = jnp.where(number < n_train_ref[0], 0.0, masked_score)
+
+    loads[2].wait()
+    loads[3].wait()
 
     def feature_rows(step, carry):
         cells = jnp.concatenate([cells_ref[step * 2 + one].T for one in range(2)], axis=0)
@@ -280,6 +297,9 @@
         return carry
 
     lax.fori_loop(0, pairs, item_pair, 0)
+
+    for load in loads[4:]:
+        load.wait()
 
     def finish(pair, carry):
         each(lambda step: returning(pair, step).wait_recv())
@@ -326,12 +346,18 @@
     bf16, f32 = jnp.bfloat16, jnp.float32
     slots = pltpu.VMEM((pairs, devices, 3 * rows, LANES), bf16)
     sems = pltpu.SemaphoreType.DMA((pairs, devices))
+    arrays = (
+        feat_qkv, item_qkv, jnp.transpose(cells, (0, 2, 1)), feat_out, item_out, mlp_in, mlp_out.T,
+    )
     return pl.pallas_call(
         functools.partial(kernel, devices),
         out_shape=jax.ShapeDtypeStruct(cells.shape, f32),
-        in_specs=[pl.BlockSpec(memory_space=pltpu.SMEM)] + [vmem] * 9,
+        in_specs=[pl.BlockSpec(memory_space=pltpu.SMEM), vmem, vmem]
+        + [pl.BlockSpec(memory_space=pltpu.HBM)] * 7,
         out_specs=vmem,
-        scratch_shapes=[
+        scratch_shapes=[pltpu.VMEM(array.shape, array.dtype) for array in arrays]
+        + [
+            pltpu.SemaphoreType.DMA((len(arrays),)),
             pltpu.VMEM((2 * width, width), bf16),
             pltpu.VMEM((width, 4 * width), bf16),
             pltpu.VMEM((2 * width, width), bf16),
@@ -344,11 +370,10 @@
             slots, slots, slots, slots, sems, sems, sems, sems,
         ],
         compiler_params=pltpu.CompilerParams(
-            collective_id=0, has_side_effects=True, vmem_limit_bytes=48 * 1024 * 1024
+            collective_id=0, has_side_effects=True, vmem_limit_bytes=62 * 1024 * 1024 + 512 * 1024
         ),
     )(
-        n_train, jnp.transpose(cells, (0, 2, 1)), present.reshape(1, feats), norm_gain, feat_qkv, feat_out, item_qkv, item_out,
-        mlp_in, mlp_out.T,
+        n_train, norm_gain, present.reshape(1, feats), *arrays
     )
 
 

time: 43.6 us -> 40.2 us (0.922)
  local copies, waits for them, and re-layouts: 8.63 us -> 2.44 us
  Pallas kernels: 33.9 us -> 36.9 us
    unnamed x18 -> x0, local copies, waits for them, and re-layouts: 7.41 us -> none
    pallas_call x1, Pallas kernels: 33.9 us -> 36.9 us  [body(): pl.pallas_call(functools.partial(kernel, devices), out_shape=jax.ShapeDty...]
    pallas_call x1, local copies, waits for them, and re-layouts: 1.22 us -> 2.44 us  [body(): pl.pallas_call(functools.partial(kernel, devices), out_shape=jax.ShapeDty...]
where the time goes in v4:
time: 40.2 us; the launch traced here: 40 us
  Pallas kernels  36.9 us (92%)
  local copies, waits for them, and re-layouts  2.44 us (6%)
  between operations  0.66 us (2%)
    pallas_call x1, Pallas kernels, body(): pl.pallas_call(functools.partial(kernel, devices), out_shape=jax.ShapeDty...  36.9 us
    pallas_call x1, local copies, waits for them, and re-layouts, body(): pl.pallas_call(functools.partial(kernel, devices), out_shape=jax.ShapeDty...  2.44 us

profile of v4, /device:TPU:0, one launch (start us, length us, event | category | flops | bytes accessed | tf_op | source)
XLA Modules:
  0.0 40.0 jit_solution(14701481932794327113)
XLA Ops:
  0.7 36.9 %shard_map.100 = f32[8,128,192]{2,1,0:T(8,128)} custom-call(s32[1]{0:T(128)S(6)} %copy.12.n_train_ref, f32[3,192]{1,0:T(4,128)} %gain_ref.1, s32[1,128]{1,0:T(1,128)} %bitcast.5, bf16[3,192,192]{2,1,0:T(8,128)(2,1)} %feat_qkv_hbm.1, bf16[3,192,192]{2,1,0:T(8,128)(2,1)} %item_qkv_hbm.1, f32[8,192,128]{2,1,0:T(8,128)} %bitcast.3, ...), custom_call_target="tpu_custom_call" | custom-call | tf_op jit(solution)/shard_map/pallas_call | solution.py:352
  37.5 2.4 %copy.11 = f32[8,128,192]{1,2,0:T(8,128)} copy(f32[8,128,192]{2,1,0:T(8,128)} %shard_map.100) | data formatting | bytes 1572864 | tf_op jit(solution)/shard_map/pallas_call | solution.py:352

commit v5 on v3

--- a/solution.py
+++ b/solution.py
@@ -165,7 +165,7 @@
     home, send_sem, recv_sem, back_sem, home_sem,
 ):
     me = lax.axis_index("row")
-    rows, width, feats = cells_ref.shape
+    rows, feats, width = cells_ref.shape
     feat_dev = feats // devices
     pairs = feat_dev // 2
     total_rows = rows * devices
@@ -200,14 +200,10 @@
     lax.fori_loop(1, devices, greet, 0)
 
     prepare_weights(feat_qkv_ref, turned_f, spread_f)
-    prepare_weights(item_qkv_ref, turned_i, spread_i)
     live = jnp.where(present_ref[...] > 0, 0.0, masked_score)
     bias_f[...] = jnp.broadcast_to(live, (feats, feats)).T
-    number = lax.broadcasted_iota(jnp.int32, (total_rows, total_rows), 0)
-    bias_i[...] = jnp.where(number < n_train_ref[0], 0.0, masked_score)
-
     def feature_rows(step, carry):
-        cells = jnp.concatenate([cells_ref[step * 2 + one].T for one in range(2)], axis=0)
+        cells = cells_ref[pl.ds(step * 2, 2)].reshape(2 * feats, width)
         normed = layer_norm(cells, gain_ref[0:1, :]).astype(jnp.bfloat16)
         contexts = attention(normed, turned_f, spread_f, bias_f)
         context = jnp.concatenate(contexts, axis=1).astype(jnp.bfloat16)
@@ -261,6 +257,10 @@
         for step in order:
             outgoing(pair, step).start()
 
+    prepare_weights(item_qkv_ref, turned_i, spread_i)
+    number = lax.broadcasted_iota(jnp.int32, (total_rows, total_rows), 0)
+    bias_i[...] = jnp.where(number < n_train_ref[0], 0.0, masked_score)
+
     def item_pair(pair, carry):
         each(lambda step: outgoing(pair, step).wait_recv())
         arrived = unpack(recv, pair)
@@ -277,11 +277,13 @@
         home[pair, me] = back[pair, me]
         for step in order:
             returning(pair, step).start()
+        each(lambda step: outgoing(pair, step).wait_send())
         return carry
 
     lax.fori_loop(0, pairs, item_pair, 0)
 
     def finish(pair, carry):
+        each(lambda step: returning(pair, step).wait_send())
         each(lambda step: returning(pair, step).wait_recv())
         context = unpack(home, pair).reshape(group, width).astype(jnp.bfloat16)
         late = mid[pair] + matmul(context, item_out_ref[...])
@@ -301,10 +303,6 @@
     for row in range(rows):
         out_ref[row, :, :LANES] = mid_a[row * feats : (row + 1) * feats, :]
         out_ref[row, :, LANES:] = mid_b[row * feats : (row + 1) * feats, :rest]
-
-    for pair in range(pairs):
-        each(lambda step: outgoing(pair, step).wait_send())
-        each(lambda step: returning(pair, step).wait_send())
 
 
 def body(
@@ -347,7 +345,7 @@
             collective_id=0, has_side_effects=True, vmem_limit_bytes=48 * 1024 * 1024
         ),
     )(
-        n_train, jnp.transpose(cells, (0, 2, 1)), present.reshape(1, feats), norm_gain, feat_qkv, feat_out, item_qkv, item_out,
+        n_train, cells, present.reshape(1, feats), norm_gain, feat_qkv, feat_out, item_qkv, item_out,
         mlp_in, mlp_out.T,
     )
 

time: 43.6 us -> 36.5 us (0.84)
  local copies, waits for them, and re-layouts: 8.63 us -> 2.81 us
  Pallas kernels: 33.9 us -> 32.8 us
    unnamed x18 -> x17, local copies, waits for them, and re-layouts: 7.41 us -> 1.59 us
    pallas_call x1, Pallas kernels: 33.9 us -> 32.8 us  [body(): pl.pallas_call(functools.partial(kernel, devices), out_shape=jax.ShapeDty...]
where the time goes in v5:
time: 36.5 us; the launch traced here: 36.4 us
  Pallas kernels  32.8 us (90%)
  local copies, waits for them, and re-layouts  2.81 us (8%)
  between operations  0.79 us (2%)
    pallas_call x1, Pallas kernels, body(): pl.pallas_call(functools.partial(kernel, devices), out_shape=jax.ShapeDty...  32.8 us
    unnamed x17, local copies, waits for them, and re-layouts  1.59 us
    pallas_call x1, local copies, waits for them, and re-layouts, body(): pl.pallas_call(functools.partial(kernel, devices), out_shape=jax.ShapeDty...  1.22 us

profile of v5, /device:TPU:0, one launch (start us, length us, event | category | flops | bytes accessed | tf_op | source)
XLA Modules:
  0.0 36.4 jit_solution(11343679824148847050)
XLA Ops:
  0.7 0.0 copy-start
  0.7 0.0 copy-start.1
  0.7 0.0 copy-start.2
  0.7 0.0 copy-start.3
  0.7 0.0 copy-start.4
  0.7 0.0 copy-start.5
  0.7 0.0 copy-start.6
  0.7 0.0 copy-start.7
  0.7 1.6 %copy.11.cells_ref = f32[8,128,192]{2,1,0:T(8,128)S(1)} copy(f32[8,128,192]{1,2,0:T(8,128)} %param.10) | data formatting | bytes 1572864 | tf_op args[0]
  2.3 0.0 copy-done
  2.3 0.0 copy-done.1
  2.3 0.0 copy-done.2
  2.3 0.0 copy-done.3
  2.3 0.0 copy-done.4
  2.3 0.0 copy-done.5
  2.4 0.0 copy-done.6
  2.4 0.0 copy-done.7
  2.4 32.8 %shard_map.100 = f32[8,128,192]{2,1,0:T(8,128)S(1)} custom-call(s32[1]{0:T(128)S(6)} %copy.13.n_train_ref, f32[8,128,192]{2,1,0:T(8,128)S(1)} %copy.11.cells_ref, s32[1,128]{1,0:T(1,128)S(1)} %bitcast.3, f32[3,192]{1,0:T(4,128)S(1)} %copy-done.6, bf16[3,192,192]{2,1,0:T(8,128)(2,1)S(1)} %copy-done, bf16[192,192]{1,0:T(8,128)(2,1)S(1)} %copy-done.4, ...), custom_call_target="tpu_custom_call" | custom-call | tf_op jit(solution)/shard_map/pallas_call | solution.py:327
  35.2 1.2 %copy.12 = f32[8,128,192]{1,2,0:T(8,128)} copy(f32[8,128,192]{2,1,0:T(8,128)S(1)} %shard_map.100) | data formatting | bytes 1572864 | tf_op jit(solution)/shard_map/pallas_call | solution.py:327
Async XLA Ops:
  0.7 1.6 %copy-start = (bf16[3,192,192]{2,1,0:T(8,128)(2,1)S(1)}, bf16[3,192,192]{2,1,0:T(8,128)(2,1)}, u32[]{:S(2)}) copy-start(bf16[3,192,192]{2,1,0:T(8,128)(2,1)} %feat_qkv_ref.1) | copy-start | bytes 663556
  0.7 1.6 %copy-start.1 = (bf16[3,192,192]{2,1,0:T(8,128)(2,1)S(1)}, bf16[3,192,192]{2,1,0:T(8,128)(2,1)}, u32[]{:S(2)}) copy-start(bf16[3,192,192]{2,1,0:T(8,128)(2,1)} %item_qkv_ref.1) | copy-start | bytes 663556
  0.7 1.6 %copy-start.2 = (bf16[192,768]{1,0:T(8,128)(2,1)S(1)}, bf16[192,768]{1,0:T(8,128)(2,1)}, u32[]{:S(2)}) copy-start(bf16[192,768]{1,0:T(8,128)(2,1)} %mlp_in_ref.1) | copy-start | bytes 884740
  0.7 1.6 %copy-start.3 = (bf16[768,192]{0,1:T(8,128)(2,1)S(1)}, bf16[768,192]{0,1:T(8,128)(2,1)}, u32[]{:S(2)}) copy-start(bf16[768,192]{0,1:T(8,128)(2,1)} %param.19) | copy-start | bytes 884740
  0.7 1.6 %copy-start.4 = (bf16[192,192]{1,0:T(8,128)(2,1)S(1)}, bf16[192,192]{1,0:T(8,128)(2,1)}, u32[]{:S(2)}) copy-start(bf16[192,192]{1,0:T(8,128)(2,1)} %feat_out_ref.1) | copy-start | bytes 221188
  0.7 1.6 %copy-start.5 = (bf16[192,192]{1,0:T(8,128)(2,1)S(1)}, bf16[192,192]{1,0:T(8,128)(2,1)}, u32[]{:S(2)}) copy-start(bf16[192,192]{1,0:T(8,128)(2,1)} %item_out_ref.1) | copy-start | bytes 221188
  0.7 1.6 %copy-start.6 = (f32[3,192]{1,0:T(4,128)S(1)}, f32[3,192]{1,0:T(4,128)}, u32[]{:S(2)}) copy-start(f32[3,192]{1,0:T(4,128)} %gain_ref.1) | copy-start | bytes 6916
  0.7 1.6 %copy-start.7 = (s32[128]{0:T(128)S(1)}, s32[128]{0:T(128)}, u32[]{:S(2)}) copy-start(s32[128]{0:T(128)} %param.12) | copy-start | bytes 1540

commit v6 on v5

--- a/solution.py
+++ b/solution.py
@@ -213,7 +213,7 @@
         mid_b[here, :rest] = updated[:, LANES:]
         return carry
 
-    lax.fori_loop(0, rows // 2, feature_rows, 0)
+    lax.fori_loop(0, rows // 2, feature_rows, 0, unroll=2)
 
     def outgoing(pair, step):
         to = lax.rem(me + step, devices)

time: 36.5 us -> 35.2 us (0.964)
  Pallas kernels: 32.8 us -> 31.4 us
    pallas_call x1, Pallas kernels: 32.8 us -> 31.4 us  [body(): pl.pallas_call(functools.partial(kernel, devices), out_shape=jax.ShapeDty...]
where the time goes in v6:
time: 35.2 us; the launch traced here: 35 us
  Pallas kernels  31.4 us (89%)
  local copies, waits for them, and re-layouts  2.81 us (8%)
  between operations  0.79 us (2%)
    pallas_call x1, Pallas kernels, body(): pl.pallas_call(functools.partial(kernel, devices), out_shape=jax.ShapeDty...  31.4 us
    unnamed x17, local copies, waits for them, and re-layouts  1.59 us
    pallas_call x1, local copies, waits for them, and re-layouts, body(): pl.pallas_call(functools.partial(kernel, devices), out_shape=jax.ShapeDty...  1.22 us

profile of v6, /device:TPU:0, one launch (start us, length us, event | category | flops | bytes accessed | tf_op | source)
XLA Modules:
  0.0 35.0 jit_solution(9610561558701363064)
XLA Ops:
  0.7 0.0 copy-start
  0.7 0.0 copy-start.1
  0.7 0.0 copy-start.2
  0.7 0.0 copy-start.3
  0.7 0.0 copy-start.4
  0.7 0.0 copy-start.5
  0.7 0.0 copy-start.6
  0.7 0.0 copy-start.7
  0.7 1.6 %copy.11.cells_ref = f32[8,128,192]{2,1,0:T(8,128)S(1)} copy(f32[8,128,192]{1,2,0:T(8,128)} %param.10) | data formatting | bytes 1572864 | tf_op args[0]
  2.3 0.0 copy-done
  2.3 0.0 copy-done.1
  2.3 0.0 copy-done.2
  2.3 0.0 copy-done.3
  2.3 0.0 copy-done.4
  2.3 0.0 copy-done.5
  2.4 0.0 copy-done.6
  2.4 0.0 copy-done.7
  2.4 31.4 %shard_map.100 = f32[8,128,192]{2,1,0:T(8,128)S(1)} custom-call(s32[1]{0:T(128)S(6)} %copy.13.n_train_ref, f32[8,128,192]{2,1,0:T(8,128)S(1)} %copy.11.cells_ref, s32[1,128]{1,0:T(1,128)S(1)} %bitcast.3, f32[3,192]{1,0:T(4,128)S(1)} %copy-done.6, bf16[3,192,192]{2,1,0:T(8,128)(2,1)S(1)} %copy-done, bf16[192,192]{1,0:T(8,128)(2,1)S(1)} %copy-done.4, ...), custom_call_target="tpu_custom_call" | custom-call | tf_op jit(solution)/shard_map/pallas_call | solution.py:327
  33.8 1.2 %copy.12 = f32[8,128,192]{1,2,0:T(8,128)} copy(f32[8,128,192]{2,1,0:T(8,128)S(1)} %shard_map.100) | data formatting | bytes 1572864 | tf_op jit(solution)/shard_map/pallas_call | solution.py:327
Async XLA Ops:
  0.7 1.6 %copy-start = (bf16[3,192,192]{2,1,0:T(8,128)(2,1)S(1)}, bf16[3,192,192]{2,1,0:T(8,128)(2,1)}, u32[]{:S(2)}) copy-start(bf16[3,192,192]{2,1,0:T(8,128)(2,1)} %feat_qkv_ref.1) | copy-start | bytes 663556
  0.7 1.6 %copy-start.1 = (bf16[3,192,192]{2,1,0:T(8,128)(2,1)S(1)}, bf16[3,192,192]{2,1,0:T(8,128)(2,1)}, u32[]{:S(2)}) copy-start(bf16[3,192,192]{2,1,0:T(8,128)(2,1)} %item_qkv_ref.1) | copy-start | bytes 663556
  0.7 1.6 %copy-start.2 = (bf16[192,768]{1,0:T(8,128)(2,1)S(1)}, bf16[192,768]{1,0:T(8,128)(2,1)}, u32[]{:S(2)}) copy-start(bf16[192,768]{1,0:T(8,128)(2,1)} %mlp_in_ref.1) | copy-start | bytes 884740
  0.7 1.6 %copy-start.3 = (bf16[768,192]{0,1:T(8,128)(2,1)S(1)}, bf16[768,192]{0,1:T(8,128)(2,1)}, u32[]{:S(2)}) copy-start(bf16[768,192]{0,1:T(8,128)(2,1)} %param.19) | copy-start | bytes 884740
  0.7 1.6 %copy-start.4 = (bf16[192,192]{1,0:T(8,128)(2,1)S(1)}, bf16[192,192]{1,0:T(8,128)(2,1)}, u32[]{:S(2)}) copy-start(bf16[192,192]{1,0:T(8,128)(2,1)} %feat_out_ref.1) | copy-start | bytes 221188
  0.7 1.6 %copy-start.5 = (bf16[192,192]{1,0:T(8,128)(2,1)S(1)}, bf16[192,192]{1,0:T(8,128)(2,1)}, u32[]{:S(2)}) copy-start(bf16[192,192]{1,0:T(8,128)(2,1)} %item_out_ref.1) | copy-start | bytes 221188
  0.7 1.6 %copy-start.6 = (f32[3,192]{1,0:T(4,128)S(1)}, f32[3,192]{1,0:T(4,128)}, u32[]{:S(2)}) copy-start(f32[3,192]{1,0:T(4,128)} %gain_ref.1) | copy-start | bytes 6916
  0.7 1.6 %copy-start.7 = (s32[128]{0:T(128)S(1)}, s32[128]{0:T(128)}, u32[]{:S(2)}) copy-start(s32[128]{0:T(128)} %param.12) | copy-start | bytes 1540
